TPU v7x, 32 devices: a whole 2x2x4 slice. The times are simulated.
32 devices in a mesh: dp: 8 (over y, x, core), mp: 4 (over z).
Axes of the slice: x: 2, y: 2, z: 4, core: 2. Of those that a mesh axis runs over, the one named last changes fastest.
Arguments:
- tokens: bfloat16 [16384, 1024], P(('dp', 'mp')), may hold values from -6 to 6
- norm_gain: float32 [2, 1024], replicated, may hold values from 0.1 to 1.9
- qkv_weight: bfloat16 [3, 1024, 1024], P(None, 'dp', 'mp')
- out_weight: bfloat16 [1024, 1024], P('mp', 'dp'), may hold values from -0.1875 to 0.1875
- variate_bias: float32 [2, 16], replicated, may hold values from -6 to 6
- ffn_weight: bfloat16 [2, 1024, 2816], P(None, 'dp', 'mp'), may hold values from -0.1875 to 0.1875
- down_weight: bfloat16 [2816, 1024], P('mp', 'dp'), may hold values from -0.109375 to 0.109375
- sample_ids: int32 [16384], P(('dp', 'mp')), may hold values from 0 to 127, as said below
- variate_ids: int32 [16384], P(('dp', 'mp')), may hold values from 0 to 15, as said below
- time_ids: int32 [16384], P(('dp', 'mp')), may hold values from 0 to 31, as said below
Outputs:
- encoded: bfloat16 [16384, 1024], P(('dp', 'mp'))
Inputs may be any that keep to these rules, and one draw needn't show every extreme that they name: `sample_ids`: within each packed sequence of 512 tokens the series numbers start at 0 and never fall; a series with v variates (1 to 16) and p patches (4 to 32) holds v * p consecutive tokens, the last series of a sequence may be cut short; some packed sequence holds 128 series of one variate and four patches each. `variate_ids`: A token's offset within its series divided by that series' patch count p. `time_ids`: A token's offset within its series modulo that series' patch count p.
All inputs are finite; a program needn't handle non-finite values.
Results may differ from a plain program's by a relative error of at most 0.017.
Values may be sent and summed in bfloat16 or wider, within the bound.
A program may use at most 128 MiB of HBM per device.

v0:
```python
import jax
import jax.numpy as jnp
from jax import lax
from jax.sharding import PartitionSpec as P

HEAD_DIM = 64
L = 512


def rms_norm(values, gain):
    wide = values.astype(jnp.float32)
    square = jnp.mean(wide * wide, axis=-1, keepdims=True)
    return (wide * lax.rsqrt(square + 1e-05) * gain[None, :]).astype(jnp.bfloat16)


def rotate(values, times):
    half = values.shape[-1] // 2
    freq = 10000.0 ** (-jnp.arange(half, dtype=jnp.float32) / half)
    angle = times.astype(jnp.float32)[:, None] * freq[None, :]
    cosine = jnp.cos(angle)[:, None, :]
    sine = jnp.sin(angle)[:, None, :]
    first = values[..., :half]
    second = values[..., half:]
    return jnp.concatenate(
        [first * cosine - second * sine, first * sine + second * cosine], axis=-1
    )


def rotated(raw, times):
    row_total, local_width = raw.shape
    turned = rotate(raw.reshape(row_total, local_width // HEAD_DIM, HEAD_DIM), times)
    return turned.reshape(row_total, local_width).astype(jnp.bfloat16)


def attend(queries, keys_rot, values, samples, variates, bias):
    row_total, local_width = queries.shape
    heads_here = local_width // HEAD_DIM
    count = row_total // L

    def one_sequence(args):
        qs, ks, vs, sample_row, variate_row = args
        scores = jnp.einsum(
            "qhd,khd->hqk", qs, ks, preferred_element_type=jnp.float32
        ) * HEAD_DIM ** (-0.5)
        same = variate_row[:, None] == variate_row[None, :]
        scores = scores + jnp.where(same[None], bias[0][:, None, None], bias[1][:, None, None])
        scores = jnp.where((sample_row[:, None] == sample_row[None, :])[None], scores, -1e30)
        top = jnp.max(scores, axis=2, keepdims=True)
        expo = jnp.exp(scores - top)
        weights = (expo / jnp.sum(expo, axis=2, keepdims=True)).astype(jnp.bfloat16)
        return jnp.einsum("hqk,khd->qhd", weights, vs, preferred_element_type=jnp.float32).astype(
            jnp.bfloat16
        )

    shape = (count, L, heads_here, HEAD_DIM)
    result = lax.map(
        one_sequence,
        (
            queries.reshape(shape),
            keys_rot.reshape(shape),
            values.reshape(shape),
            samples.reshape(count, L),
            variates.reshape(count, L),
        ),
    )
    return result.reshape(row_total, local_width)


def local(
    tokens,
    norm_gain,
    qkv_weight,
    out_weight,
    variate_bias,
    ffn_weight,
    down_weight,
    sample_ids,
    variate_ids,
    time_ids,
):
    heads_here = qkv_weight.shape[2] // HEAD_DIM
    head_start = lax.axis_index("mp") * heads_here
    bias_local = lax.dynamic_slice_in_dim(variate_bias, head_start, heads_here, 1)
    first_normed = rms_norm(tokens, norm_gain[0])
    wide_columns = lax.all_gather(qkv_weight, "mp", axis=2, tiled=True)
    columns = first_normed
    projected = jnp.einsum(
        "rc,jcd->jrd",
        columns,
        lax.all_gather(wide_columns, "dp", axis=1, tiled=True),
        preferred_element_type=jnp.float32,
    )
    queries = rotated(projected[0], time_ids)
    keys_rot = rotated(projected[1], time_ids)
    values = projected[2].astype(jnp.bfloat16)
    grouped = lax.all_to_all(
        jnp.stack([queries, keys_rot, values]), "mp", split_axis=2, concat_axis=1, tiled=True
    )
    gathered_ids = (
        lax.all_gather(sample_ids, "mp", axis=0, tiled=True),
        lax.all_gather(variate_ids, "mp", axis=0, tiled=True),
    )
    attended = attend(
        grouped[0], grouped[1], grouped[2], gathered_ids[0], gathered_ids[1], bias_local
    )
    back_rows = lax.all_to_all(attended, "mp", split_axis=0, concat_axis=1, tiled=True)
    out_rows = lax.all_gather(out_weight, "mp", axis=0, tiled=True)
    mixed = jnp.dot(
        back_rows,
        lax.all_gather(out_rows, "dp", axis=1, tiled=True),
        preferred_element_type=jnp.float32,
    )
    residual = (tokens.astype(jnp.float32) + mixed).astype(jnp.bfloat16)
    second_normed = rms_norm(residual, norm_gain[1])
    ffn_columns = lax.all_gather(ffn_weight, "mp", axis=2, tiled=True)
    columns = second_normed
    gate_up = jnp.einsum(
        "rc,jcf->jrf",
        columns,
        lax.all_gather(ffn_columns, "dp", axis=1, tiled=True),
        preferred_element_type=jnp.float32,
    )
    hidden = (jax.nn.silu(gate_up[0]) * gate_up[1]).astype(jnp.bfloat16)
    down_full = lax.all_gather(down_weight, "mp", axis=0, tiled=True)
    feed = jnp.dot(
        hidden,
        lax.all_gather(down_full, "dp", axis=1, tiled=True),
        preferred_element_type=jnp.float32,
    )
    return (residual.astype(jnp.float32) + feed).astype(jnp.bfloat16)


def solution(mesh):
    return jax.shard_map(
        local,
        mesh=mesh,
        in_specs=(
            P(("dp", "mp"), None),
            P(),
            P(None, "dp", "mp"),
            P("mp", "dp"),
            P(),
            P(None, "dp", "mp"),
            P("mp", "dp"),
            P(("dp", "mp")),
            P(("dp", "mp")),
            P(("dp", "mp")),
        ),
        out_specs=P(("dp", "mp"), None),
        check_vma=False,
    )
```

profile of v0, /device:TPU:0, one launch (start us, length us, event | category | flops | bytes accessed | tf_op | source)
XLA Modules:
  0.0 358.3 jit_solution(14907393396261247635)
XLA Ops:
  8.8 27.7 %all_gather.30 = bf16[3,128,1024]{2,1,0:T(8,128)(2,1)} all-gather(bf16[3,128,256]{2,1,0:T(8,128)(2,1)} %param.14), channel_id=1, replica_groups=mesh['dp'=8,'mp'=4] {'mp'}, dimensions={2}, use_global_device_ids=true | all-gather | bytes 983040 | tf_op jit(solution)/shard_map/all_gather | solution.py:85
  36.6 18.9 %all_gather.34 = bf16[1024,128]{1,0:T(8,128)(2,1)} all-gather(bf16[256,128]{1,0:T(8,128)(2,1)} %param.15), channel_id=1, replica_groups=mesh['dp'=8,'mp'=4] {'mp'}, dimensions={0}, use_global_device_ids=true | all-gather | bytes 327680 | tf_op jit(solution)/shard_map/all_gather | solution.py:107
  56.8 4.9 %copy.41 = bf16[2,128,2816]{2,1,0:T(8,128)(2,1)} copy(bf16[2,128,2816]{1,0,2:T(2,128)(2,1)} %all-gather.12.cloned.1.call-done) | data formatting | bytes 2883584 | tf_op jit(solution)/shard_map/all_gather | solution.py:115
  62.3 41.2 %all-gather.8.cloned.1.call-done = bf16[3,1024,1024]{2,1,0:T(8,128)(2,1)} async-done(((bf16[3,128,1024]{2,1,0:T(8,128)(2,1)}), bf16[3,1024,1024]{2,1,0:T(8,128)(2,1)}) %all-gather.8.cloned.1.call-update) | async-done | bytes 6291472 | tf_op jit(solution)/shard_map/all_gather | solution.py:90
  103.5 5.7 %convolution_bitcast_fusion.1 = f32[3,512,1024]{2,1,0:T(8,128)S(1)} fusion(bf16[3,1024,1024]{2,1,0:T(8,128)(2,1)} %all-gather.8.cloned.1.call-done, bf16[512,1024]{1,0:T(8,128)(2,1)S(1)} %copy-done.2, f32[1024]{0:T(1024)S(1)} %bitcast.128, f32[512]{0:T(512)S(1)} %add_rsqrt_fusion.1), kind=kOutput, calls=%fused_computation.54 | convolution fusion | flops 3223322624 | bytes 13637632 | tf_op jit(solution)/shard_map/rc,jcd->jrd/dot_general | solution.py:87
  125.3 5.7 %copy.38 = bf16[3,512,1024]{1,0,2:T(4,128)(2,1)} copy(bf16[3,512,1024]{2,1,0:T(8,128)(2,1)S(1)} %pad_maximum_fusion) | data formatting | bytes 6291456 | tf_op jit(solution)/shard_map/stack | solution.py:97
  131.0 5.0 %all-to-all-start = ((bf16[3,512,1024]{1,0,2:T(4,128)(2,1)}), bf16[3,512,1024]{1,0,2:T(4,128)(2,1)}, u32[]{:S(2)}, u32[]{:S(2)}) async-start(bf16[3,512,1024]{1,0,2:T(4,128)(2,1)} %copy.38), calls=%async_computation | async-start | bytes 8388608 | tf_op jit(solution)/shard_map/all_to_all | solution.py:96
  136.1 106.7 %all_gather.38 = bf16[2816,128]{1,0:T(8,128)(2,1)} all-gather(bf16[704,128]{1,0:T(8,128)(2,1)S(1)} %copy-done.4), channel_id=1, replica_groups=mesh['dp'=8,'mp'=4] {'mp'}, dimensions={0}, use_global_device_ids=true | all-gather | bytes 901120 | tf_op jit(solution)/shard_map/all_gather | solution.py:124
  242.9 11.9 %all-gather.1 = s32[4,1,512]{2,1,0:T(1,128)S(1)} all-gather(s32[1,1,512]{2,1,0:T(1,128)S(1)} %bitcast.129), channel_id=1, replica_groups=mesh['dp'=8,'mp'=4] {'mp'}, dimensions={0}, use_global_device_ids=true | all-gather | bytes 10240 | tf_op jit(solution)/shard_map/all_gather | solution.py:101
  254.8 12.1 %all-gather = s32[4,1,512]{2,1,0:T(1,128)S(1)} all-gather(s32[1,1,512]{2,1,0:T(1,128)S(1)} %bitcast.130), channel_id=1, replica_groups=mesh['dp'=8,'mp'=4] {'mp'}, dimensions={0}, use_global_device_ids=true | all-gather | bytes 10240 | tf_op jit(solution)/shard_map/all_gather | solution.py:100
  267.0 3.2 copy.39
  271.7 31.2 %while.10 = (s32[]{:T(128)}, bf16[4,512,4,64]{1,3,2,0:T(8,128)(2,1)}, bf16[4,512,4,64]{1,3,2,0:T(8,128)(2,1)}, s32[4,512]{1,0:T(4,128)S(1)}, bf16[4,512,4,64]{1,...) while((s32[]{:T(128)}, ...), condition=%wide.region_4.5_spmd, body=%wide.region_1.4_spmd.sunk | while | flops 416943104 | bytes 3179681 | solution.py:56
  272.2 3.0 fusion.100
  275.2 4.3 %fusion.101 = bf16[4,512,4,64]{1,3,2,0:T(8,128)(2,1)} fusion(bf16[4,512,4,64]{1,3,2,0:T(8,128)(2,1)} %get-tuple-element.154, s32[]{:T(128)} %get-tuple-element.153, f32[4,512]{1,0:T(4,128)S(1)} %fusion.100, bf16[4,512,4,64]{1,3,2,0:T(8,128)(2,1)} %get-tuple-element.164, f32[4]{0:T(128)S(1)} %get-tuple-element.140, f32[4]{0:T(128)S(1)} %get-tuple-element.141, ...), kind=kOutput, calls=%fused_computation.14.clone.1 | convolution fusion | flops 275909120 | bytes 1584128 | tf_op jit(solution)/shard_map/while/body/eval_jaxpr/hqk,khd->qhd/dot_general | solution.py:51
  280.0 3.0 fusion.100
  283.0 4.3 %fusion.101 = bf16[4,512,4,64]{1,3,2,0:T(8,128)(2,1)} fusion(bf16[4,512,4,64]{1,3,2,0:T(8,128)(2,1)} %get-tuple-element.154, s32[]{:T(128)} %get-tuple-element.153, f32[4,512]{1,0:T(4,128)S(1)} %fusion.100, bf16[4,512,4,64]{1,3,2,0:T(8,128)(2,1)} %get-tuple-element.164, f32[4]{0:T(128)S(1)} %get-tuple-element.140, f32[4]{0:T(128)S(1)} %get-tuple-element.141, ...), kind=kOutput, calls=%fused_computation.14.clone.1 | convolution fusion | flops 275909120 | bytes 1584128 | tf_op jit(solution)/shard_map/while/body/eval_jaxpr/hqk,khd->qhd/dot_general | solution.py:51
  287.8 3.0 fusion.100
  290.8 4.3 %fusion.101 = bf16[4,512,4,64]{1,3,2,0:T(8,128)(2,1)} fusion(bf16[4,512,4,64]{1,3,2,0:T(8,128)(2,1)} %get-tuple-element.154, s32[]{:T(128)} %get-tuple-element.153, f32[4,512]{1,0:T(4,128)S(1)} %fusion.100, bf16[4,512,4,64]{1,3,2,0:T(8,128)(2,1)} %get-tuple-element.164, f32[4]{0:T(128)S(1)} %get-tuple-element.140, f32[4]{0:T(128)S(1)} %get-tuple-element.141, ...), kind=kOutput, calls=%fused_computation.14.clone.1 | convolution fusion | flops 275909120 | bytes 1584128 | tf_op jit(solution)/shard_map/while/body/eval_jaxpr/hqk,khd->qhd/dot_general | solution.py:51
  295.6 3.0 fusion.100
  298.6 4.3 %fusion.101 = bf16[4,512,4,64]{1,3,2,0:T(8,128)(2,1)} fusion(bf16[4,512,4,64]{1,3,2,0:T(8,128)(2,1)} %get-tuple-element.154, s32[]{:T(128)} %get-tuple-element.153, f32[4,512]{1,0:T(4,128)S(1)} %fusion.100, bf16[4,512,4,64]{1,3,2,0:T(8,128)(2,1)} %get-tuple-element.164, f32[4]{0:T(128)S(1)} %get-tuple-element.140, f32[4]{0:T(128)S(1)} %get-tuple-element.141, ...), kind=kOutput, calls=%fused_computation.14.clone.1 | convolution fusion | flops 275909120 | bytes 1584128 | tf_op jit(solution)/shard_map/while/body/eval_jaxpr/hqk,khd->qhd/dot_general | solution.py:51
  302.9 3.7 %all-to-all-start.1 = ((bf16[4,512,256]{1,2,0:T(8,128)(2,1)}), bf16[4,512,256]{1,2,0:T(8,128)(2,1)S(1)}, u32[]{:S(2)}, u32[]{:S(2)}) async-start(bf16[4,512,256]{1,2,0:T(8,128)(2,1)} %bitcast.24), calls=%async_computation.1 | async-start | bytes 2097152 | tf_op jit(solution)/shard_map/all_to_all | solution.py:106
  306.7 18.6 %all-to-all-done.1 = bf16[4,512,256]{1,2,0:T(8,128)(2,1)S(1)} async-done(((bf16[4,512,256]{1,2,0:T(8,128)(2,1)}), bf16[4,512,256]{1,2,0:T(8,128)(2,1)S(1)}, u32[]{:S(2)}, u32[]{:S(2)}) %all-to-all-start.1) | async-done | bytes 1048608 | tf_op jit(solution)/shard_map/all_to_all | solution.py:106
  328.3 13.2 %convolution_bitcast_fusion = f32[2,512,2816]{2,1,0:T(8,128)} fusion(bf16[2,1024,2816]{2,1,0:T(8,128)(2,1)} %all-gather.14.cloned.1.call-done, bf16[512,1024]{1,0:T(8,128)(2,1)S(1)} %get-tuple-element.84, f32[1024]{0:T(1024)S(1)} %bitcast.125, f32[512]{0:T(512)S(1)} %add_rsqrt_fusion), kind=kOutput, calls=%fused_computation.41 | convolution fusion | flops 5907677184 | bytes 24123392 | tf_op jit(solution)/shard_map/rc,jcf->jrf/dot_general | solution.py:117
  341.6 10.2 %fusion.63 = bf16[512,1024]{1,0:T(8,128)(2,1)} fusion(bf16[512,1024]{1,0:T(8,128)(2,1)S(1)} %get-tuple-element.84, bf16[2816,1024]{1,0:T(8,128)(2,1)} %all-gather.16.cloned.1.call-done, f32[2,512,2816]{2,1,0:T(8,128)} %convolution_bitcast_fusion), kind=kOutput, calls=%fused_computation.62 | convolution fusion | flops 2963013632 | bytes 19398656 | tf_op jit(solution)/shard_map/dot_general | solution.py:125
  (72 shorter events, 26.8 us)
Async XLA Ops:
  6.5 260.4 %copy-start = (f32[2,16]{1,0:T(2,128)S(1)}, f32[2,16]{1,0:T(2,128)}, u32[]{:S(2)}) copy-start(f32[2,16]{1,0:T(2,128)} %param.16) | copy-start | bytes 388
  6.5 55.1 %copy-start.8 = (s32[512]{0:T(512)S(1)}, s32[512]{0:T(512)}, u32[]{:S(2)}) copy-start(s32[512]{0:T(512)} %param.21) | copy-start | bytes 6148
  6.5 55.2 %copy-start.2 = (bf16[512,1024]{1,0:T(8,128)(2,1)S(1)}, bf16[512,1024]{1,0:T(8,128)(2,1)}, u32[]{:S(2)}) copy-start(bf16[512,1024]{1,0:T(8,128)(2,1)} %param.12) | copy-start | bytes 3145732
  6.5 50.2 %all-gather.12.cloned.1.call-start = ((), (), s32[]{:S(2)}) async-start(), calls=%async_computation.4 | async-start | bytes 1802240 | tf_op jit(solution)/shard_map/all_gather | solution.py:115
  8.7 53.3 %copy-start.5 = (f32[2,1024]{1,0:T(2,128)S(1)}, f32[2,1024]{1,0:T(2,128)}, u32[]{:S(2)}) copy-start(f32[2,1024]{1,0:T(2,128)} %param.13) | copy-start | bytes 24580
  8.8 94.8 %all-gather.8.cloned.1.call-start = ((), (), s32[]{:S(2)}) async-start(), calls=%async_computation.2 | async-start | bytes 7077888 | tf_op jit(solution)/shard_map/all_gather | solution.py:90
  36.5 270.2 %all-gather.10.cloned.1.call-start = ((), (), s32[]{:S(2)}) async-start(), calls=%async_computation.3 | async-start | bytes 2359296 | tf_op jit(solution)/shard_map/all_gather | solution.py:110
  55.5 272.8 %all-gather.14.cloned.1.call-start = ((), (), s32[]{:S(2)}) async-start(), calls=%async_computation.5 | async-start | bytes 12976128 | tf_op jit(solution)/shard_map/all_gather | solution.py:120
  131.0 5.1 %copy-start.4 = (bf16[704,128]{1,0:T(8,128)(2,1)S(1)}, bf16[704,128]{1,0:T(8,128)(2,1)}, u32[]{:S(2)}) copy-start(bf16[704,128]{1,0:T(8,128)(2,1)} %param.18) | copy-start | bytes 540676
  131.0 111.8 %copy-start.6 = (s32[512]{0:T(512)S(1)}, s32[512]{0:T(512)}, u32[]{:S(2)}) copy-start(s32[512]{0:T(512)} %param.20) | copy-start | bytes 6148
  131.0 123.8 %copy-start.7 = (s32[512]{0:T(512)S(1)}, s32[512]{0:T(512)}, u32[]{:S(2)}) copy-start(s32[512]{0:T(512)} %param.19) | copy-start | bytes 6148
  131.0 136.0 %all-to-all-start = ((bf16[3,512,1024]{1,0,2:T(4,128)(2,1)}), bf16[3,512,1024]{1,0,2:T(4,128)(2,1)}, u32[]{:S(2)}, u32[]{:S(2)}) async-start(bf16[3,512,1024]{1,0,2:T(4,128)(2,1)} %copy.38), calls=%async_computation | async-start | bytes 8388608 | tf_op jit(solution)/shard_map/all_to_all | solution.py:96
  136.0 205.6 %all-gather.16.cloned.1.call-start = ((), (), s32[]{:S(2)}) async-start(), calls=%async_computation.6 | async-start | bytes 6488064 | tf_op jit(solution)/shard_map/all_gather | solution.py:127
  271.7 53.6 %copy-start.3 = (bf16[512,1024]{1,0:T(8,128)(2,1)S(1)}, bf16[512,1024]{1,0:T(8,128)(2,1)}, u32[]{:S(2)}) copy-start(bf16[512,1024]{1,0:T(8,128)(2,1)} %param.12) | copy-start | bytes 3145732
  302.9 22.3 %all-to-all-start.1 = ((bf16[4,512,256]{1,2,0:T(8,128)(2,1)}), bf16[4,512,256]{1,2,0:T(8,128)(2,1)S(1)}, u32[]{:S(2)}, u32[]{:S(2)}) async-start(bf16[4,512,256]{1,2,0:T(8,128)(2,1)} %bitcast.24), calls=%async_computation.1 | async-start | bytes 2097152 | tf_op jit(solution)/shard_map/all_to_all | solution.py:106
  341.6 10.2 %copy-start.1 = (f32[2,16]{1,0:T(2,128)S(1)}, f32[2,16]{1,0:T(2,128)}, u32[]{:S(2)}) copy-start(f32[2,16]{1,0:T(2,128)} %param.16) | copy-start | bytes 388
Sparse Core Ops, SparseCore 0:
  8.9 47.8 all-gather.11
  58.7 44.7 all-gather.7
  105.4 28.0 all-gather.9
  135.3 67.5 all-gather.13
  243.0 44.4 all-gather.15
where the time goes:
time: 359 us; the launch traced here: 358 us
  blocking collectives  177 us (49%)
  matrix products  61.5 us (17%)
  waiting for transfers between devices  61.1 us (17%)
  local copies, waits for them, and re-layouts  28.7 us (8%)
  between operations  13.3 us (4%)
  starting transfers between devices  8.9 us (2%)
  other arithmetic  7.24 us (2%)
    all_gather x1, blocking collectives, local(): down_full = lax.all_gather(down_weight, 'mp', axis=0, tiled=True)  107 us
    all_gather x1, waiting for transfers between devices, local(): lax.all_gather(wide_columns, 'dp', axis=1, tiled=True)  41.2 us
    all_gather x1, blocking collectives, local(): wide_columns = lax.all_gather(qkv_weight, 'mp', axis=2, tiled=True)  27.7 us
    all_gather x1, blocking collectives, local(): out_rows = lax.all_gather(out_weight, 'mp', axis=0, tiled=True)  18.9 us
    all_to_all x1, waiting for transfers between devices, local(): lax.all_to_all(attended, 'mp', split_axis=0, concat_axis=1, tiled=True)  18.6 us
    dot_general x4, matrix products, one_sequence(): jnp.einsum('hqk,khd->qhd', weights, vs, preferred_element_type=jnp.float32)  17.2 us
    dot_general x1, matrix products, local(): jnp.einsum('rc,jcf->jrf', columns, lax.all_gather(ffn_columns, 'dp', axis...  13.2 us
    sub x4, matrix products, one_sequence(): expo = jnp.exp(scores - top)  12.1 us
  transfers between devices with their start and end apart: 7, of which 3 were waited for; matrix products, arithmetic and copies ran while one was open for 24% of the time, Pallas kernels for 0%

commit v1 on v0

--- a/solution.py
+++ b/solution.py
@@ -105,10 +105,13 @@
     )
     back_rows = lax.all_to_all(attended, "mp", split_axis=0, concat_axis=1, tiled=True)
     out_rows = lax.all_gather(out_weight, "mp", axis=0, tiled=True)
+
+    def deliver_series_all(z_in, axis_tag):
+        plain = jax.lax.all_gather(z_in, axis_tag)
+        return jnp.concatenate(plain, axis=1)
+
     mixed = jnp.dot(
-        back_rows,
-        lax.all_gather(out_rows, "dp", axis=1, tiled=True),
-        preferred_element_type=jnp.float32,
+        back_rows, deliver_series_all(out_rows, "dp"), preferred_element_type=jnp.float32
     )
     residual = (tokens.astype(jnp.float32) + mixed).astype(jnp.bfloat16)
     second_normed = rms_norm(residual, norm_gain[1])

time: 359 us -> 356 us (level)
  matrix products: 61.5 us -> 57.4 us
    sub x4, matrix products: 12.1 us -> 8.39 us  [one_sequence(): expo = jnp.exp(scores - top)]
where the time goes in v1:
time: 356 us; the launch traced here: 355 us
  blocking collectives  177 us (50%)
  waiting for transfers between devices  58.3 us (16%)
  matrix products  57.4 us (16%)
  local copies, waits for them, and re-layouts  32.2 us (9%)
  between operations  13.3 us (4%)
  starting transfers between devices  8.9 us (2%)
  other arithmetic  7.3 us (2%)
    all_gather x1, blocking collectives, local(): down_full = lax.all_gather(down_weight, 'mp', axis=0, tiled=True)  107 us
    all_gather x1, waiting for transfers between devices, local(): lax.all_gather(wide_columns, 'dp', axis=1, tiled=True)  41.2 us
    all_gather x1, blocking collectives, local(): wide_columns = lax.all_gather(qkv_weight, 'mp', axis=2, tiled=True)  27.7 us
    all_gather x1, blocking collectives, local(): out_rows = lax.all_gather(out_weight, 'mp', axis=0, tiled=True)  18.9 us
    dot_general x4, matrix products, one_sequence(): jnp.einsum('hqk,khd->qhd', weights, vs, preferred_element_type=jnp.float32)  16.9 us
    all_to_all x1, waiting for transfers between devices, local(): lax.all_to_all(attended, 'mp', split_axis=0, concat_axis=1, tiled=True)  15.7 us
    dot_general x1, matrix products, local(): jnp.einsum('rc,jcf->jrf', columns, lax.all_gather(ffn_columns, 'dp', axis...  13.2 us
    all_gather x1, blocking collectives, local(): lax.all_gather(sample_ids, 'mp', axis=0, tiled=True)  12.1 us
  transfers between devices with their start and end apart: 7, of which 3 were waited for; matrix products, arithmetic and copies ran while one was open for 24% of the time, Pallas kernels for 0%

profile of v1, /device:TPU:0, one launch (start us, length us, event | category | flops | bytes accessed | tf_op | source)
XLA Modules:
  0.0 354.9 jit_solution(12842004485942888871)
XLA Ops:
  8.8 27.7 %all_gather.33 = bf16[3,128,1024]{2,1,0:T(8,128)(2,1)} all-gather(bf16[3,128,256]{2,1,0:T(8,128)(2,1)} %param.14), channel_id=1, replica_groups=mesh['dp'=8,'mp'=4] {'mp'}, dimensions={2}, use_global_device_ids=true | all-gather | bytes 983040 | tf_op jit(solution)/shard_map/all_gather | solution.py:85
  36.6 18.9 %all_gather.37 = bf16[1024,128]{1,0:T(8,128)(2,1)} all-gather(bf16[256,128]{1,0:T(8,128)(2,1)} %param.15), channel_id=1, replica_groups=mesh['dp'=8,'mp'=4] {'mp'}, dimensions={0}, use_global_device_ids=true | all-gather | bytes 327680 | tf_op jit(solution)/shard_map/all_gather | solution.py:107
  56.8 4.9 %copy.53 = bf16[2,128,2816]{2,1,0:T(8,128)(2,1)} copy(bf16[2,128,2816]{1,0,2:T(2,128)(2,1)} %all-gather.11.cloned.1.call-done) | data formatting | bytes 2883584 | tf_op jit(solution)/shard_map/all_gather | solution.py:118
  62.3 41.2 %all-gather.9.cloned.1.call-done = bf16[3,1024,1024]{2,1,0:T(8,128)(2,1)} async-done(((bf16[3,128,1024]{2,1,0:T(8,128)(2,1)}), bf16[3,1024,1024]{2,1,0:T(8,128)(2,1)}) %all-gather.9.cloned.1.call-update) | async-done | bytes 6291472 | tf_op jit(solution)/shard_map/all_gather | solution.py:90
  103.5 5.7 %convolution_bitcast_fusion.1 = f32[3,512,1024]{2,1,0:T(8,128)S(1)} fusion(bf16[3,1024,1024]{2,1,0:T(8,128)(2,1)} %all-gather.9.cloned.1.call-done, bf16[512,1024]{1,0:T(8,128)(2,1)S(1)} %copy-done.2, f32[1024]{0:T(1024)S(1)} %bitcast.134, f32[512]{0:T(512)S(1)} %add_rsqrt_fusion.1), kind=kOutput, calls=%fused_computation.54 | convolution fusion | flops 3223322624 | bytes 13637632 | tf_op jit(solution)/shard_map/rc,jcd->jrd/dot_general | solution.py:87
  114.8 2.9 copy.46
  122.8 2.5 pad_maximum_fusion
  125.4 5.7 %copy.49 = bf16[3,512,1024]{1,0,2:T(4,128)(2,1)} copy(bf16[3,512,1024]{2,1,0:T(8,128)(2,1)S(1)} %pad_maximum_fusion) | data formatting | bytes 6291456 | tf_op jit(solution)/shard_map/stack | solution.py:97
  131.1 5.0 %all-to-all-start = ((bf16[3,512,1024]{1,0,2:T(4,128)(2,1)}), bf16[3,512,1024]{1,0,2:T(4,128)(2,1)}, u32[]{:S(2)}, u32[]{:S(2)}) async-start(bf16[3,512,1024]{1,0,2:T(4,128)(2,1)} %copy.49), calls=%async_computation | async-start | bytes 8388608 | tf_op jit(solution)/shard_map/all_to_all | solution.py:96
  136.2 106.7 %all_gather.42 = bf16[2816,128]{1,0:T(8,128)(2,1)} all-gather(bf16[704,128]{1,0:T(8,128)(2,1)S(1)} %copy-done.4), channel_id=1, replica_groups=mesh['dp'=8,'mp'=4] {'mp'}, dimensions={0}, use_global_device_ids=true | all-gather | bytes 901120 | tf_op jit(solution)/shard_map/all_gather | solution.py:127
  242.9 11.9 %all-gather.2 = s32[4,1,512]{2,1,0:T(1,128)S(1)} all-gather(s32[1,1,512]{2,1,0:T(1,128)S(1)} %bitcast.135), channel_id=1, replica_groups=mesh['dp'=8,'mp'=4] {'mp'}, dimensions={0}, use_global_device_ids=true | all-gather | bytes 10240 | tf_op jit(solution)/shard_map/all_gather | solution.py:101
  254.9 12.1 %all-gather.1 = s32[4,1,512]{2,1,0:T(1,128)S(1)} all-gather(s32[1,1,512]{2,1,0:T(1,128)S(1)} %bitcast.136), channel_id=1, replica_groups=mesh['dp'=8,'mp'=4] {'mp'}, dimensions={0}, use_global_device_ids=true | all-gather | bytes 10240 | tf_op jit(solution)/shard_map/all_gather | solution.py:100
  267.1 3.2 copy.50
  271.4 27.1 %while.10 = (s32[]{:T(128)}, bf16[4,512,4,64]{1,3,2,0:T(8,128)(2,1)}, bf16[4,512,4,64]{1,3,2,0:T(8,128)(2,1)}, s32[4,512]{1,0:T(4,128)S(1)}, bf16[4,512,4,64]{1,...) while((s32[]{:T(128)}, ...), condition=%wide.region_4.5_spmd, body=%wide.region_1.4_spmd.sunk | while | flops 416943104 | bytes 3179681 | solution.py:56
  274.0 4.2 %fusion.101 = bf16[4,512,4,64]{1,3,2,0:T(8,128)(2,1)} fusion(bf16[4,512,4,64]{1,3,2,0:T(8,128)(2,1)} %get-tuple-element.154, s32[]{:T(128)} %get-tuple-element.153, f32[4,512]{1,0:T(4,128)S(1)} %fusion.100, bf16[4,512,4,64]{1,3,2,0:T(8,128)(2,1)} %get-tuple-element.164, f32[4]{0:T(128)S(1)} %get-tuple-element.140, f32[4]{0:T(128)S(1)} %get-tuple-element.141, ...), kind=kOutput, calls=%fused_computation.14.clone.1 | convolution fusion | flops 275909120 | bytes 1584128 | tf_op jit(solution)/shard_map/while/body/eval_jaxpr/hqk,khd->qhd/dot_general | solution.py:51
  280.8 4.2 %fusion.101 = bf16[4,512,4,64]{1,3,2,0:T(8,128)(2,1)} fusion(bf16[4,512,4,64]{1,3,2,0:T(8,128)(2,1)} %get-tuple-element.154, s32[]{:T(128)} %get-tuple-element.153, f32[4,512]{1,0:T(4,128)S(1)} %fusion.100, bf16[4,512,4,64]{1,3,2,0:T(8,128)(2,1)} %get-tuple-element.164, f32[4]{0:T(128)S(1)} %get-tuple-element.140, f32[4]{0:T(128)S(1)} %get-tuple-element.141, ...), kind=kOutput, calls=%fused_computation.14.clone.1 | convolution fusion | flops 275909120 | bytes 1584128 | tf_op jit(solution)/shard_map/while/body/eval_jaxpr/hqk,khd->qhd/dot_general | solution.py:51
  287.5 4.2 %fusion.101 = bf16[4,512,4,64]{1,3,2,0:T(8,128)(2,1)} fusion(bf16[4,512,4,64]{1,3,2,0:T(8,128)(2,1)} %get-tuple-element.154, s32[]{:T(128)} %get-tuple-element.153, f32[4,512]{1,0:T(4,128)S(1)} %fusion.100, bf16[4,512,4,64]{1,3,2,0:T(8,128)(2,1)} %get-tuple-element.164, f32[4]{0:T(128)S(1)} %get-tuple-element.140, f32[4]{0:T(128)S(1)} %get-tuple-element.141, ...), kind=kOutput, calls=%fused_computation.14.clone.1 | convolution fusion | flops 275909120 | bytes 1584128 | tf_op jit(solution)/shard_map/while/body/eval_jaxpr/hqk,khd->qhd/dot_general | solution.py:51
  294.3 4.2 %fusion.101 = bf16[4,512,4,64]{1,3,2,0:T(8,128)(2,1)} fusion(bf16[4,512,4,64]{1,3,2,0:T(8,128)(2,1)} %get-tuple-element.154, s32[]{:T(128)} %get-tuple-element.153, f32[4,512]{1,0:T(4,128)S(1)} %fusion.100, bf16[4,512,4,64]{1,3,2,0:T(8,128)(2,1)} %get-tuple-element.164, f32[4]{0:T(128)S(1)} %get-tuple-element.140, f32[4]{0:T(128)S(1)} %get-tuple-element.141, ...), kind=kOutput, calls=%fused_computation.14.clone.1 | convolution fusion | flops 275909120 | bytes 1584128 | tf_op jit(solution)/shard_map/while/body/eval_jaxpr/hqk,khd->qhd/dot_general | solution.py:51
  298.5 3.7 %all-to-all-start.1 = ((bf16[4,512,256]{1,2,0:T(8,128)(2,1)}), bf16[4,512,256]{1,2,0:T(8,128)(2,1)S(1)}, u32[]{:S(2)}, u32[]{:S(2)}) async-start(bf16[4,512,256]{1,2,0:T(8,128)(2,1)} %bitcast.24), calls=%async_computation.1 | async-start | bytes 2097152 | tf_op jit(solution)/shard_map/all_to_all | solution.py:106
  302.3 2.9 copy.51
  305.2 15.7 %all-to-all-done.1 = bf16[4,512,256]{1,2,0:T(8,128)(2,1)S(1)} async-done(((bf16[4,512,256]{1,2,0:T(8,128)(2,1)}), bf16[4,512,256]{1,2,0:T(8,128)(2,1)S(1)}, u32[]{:S(2)}, u32[]{:S(2)}) %all-to-all-start.1) | async-done | bytes 1048608 | tf_op jit(solution)/shard_map/all_to_all | solution.py:106
  321.9 3.0 fusion.60
  324.9 13.2 %convolution_bitcast_fusion = f32[2,512,2816]{2,1,0:T(8,128)} fusion(bf16[2,1024,2816]{2,1,0:T(8,128)(2,1)} %all-gather.13.cloned.1.call-done, bf16[512,1024]{1,0:T(8,128)(2,1)S(1)} %get-tuple-element.84, f32[1024]{0:T(1024)S(1)} %bitcast.131, f32[512]{0:T(512)S(1)} %add_rsqrt_fusion), kind=kOutput, calls=%fused_computation.41 | convolution fusion | flops 5907677184 | bytes 24123392 | tf_op jit(solution)/shard_map/rc,jcf->jrf/dot_general | solution.py:120
  338.2 10.2 %fusion.63 = bf16[512,1024]{1,0:T(8,128)(2,1)} fusion(bf16[512,1024]{1,0:T(8,128)(2,1)S(1)} %get-tuple-element.84, bf16[2816,1024]{1,0:T(8,128)(2,1)} %all-gather.15.cloned.1.call-done, f32[2,512,2816]{2,1,0:T(8,128)} %convolution_bitcast_fusion), kind=kOutput, calls=%fused_computation.62 | convolution fusion | flops 2963013632 | bytes 19398656 | tf_op jit(solution)/shard_map/dot_general | solution.py:128
  (73 shorter events, 27.4 us)
Async XLA Ops:
  6.5 260.5 %copy-start = (f32[2,16]{1,0:T(2,128)S(1)}, f32[2,16]{1,0:T(2,128)}, u32[]{:S(2)}) copy-start(f32[2,16]{1,0:T(2,128)} %param.16) | copy-start | bytes 388
  6.5 55.1 %copy-start.8 = (s32[512]{0:T(512)S(1)}, s32[512]{0:T(512)}, u32[]{:S(2)}) copy-start(s32[512]{0:T(512)} %param.21) | copy-start | bytes 6148
  6.5 55.2 %copy-start.2 = (bf16[512,1024]{1,0:T(8,128)(2,1)S(1)}, bf16[512,1024]{1,0:T(8,128)(2,1)}, u32[]{:S(2)}) copy-start(bf16[512,1024]{1,0:T(8,128)(2,1)} %param.12) | copy-start | bytes 3145732
  6.5 50.2 %all-gather.11.cloned.1.call-start = ((), (), s32[]{:S(2)}) async-start(), calls=%async_computation.3 | async-start | bytes 1802240 | tf_op jit(solution)/shard_map/all_gather | solution.py:118
  8.7 53.3 %copy-start.5 = (f32[2,1024]{1,0:T(2,128)S(1)}, f32[2,1024]{1,0:T(2,128)}, u32[]{:S(2)}) copy-start(f32[2,1024]{1,0:T(2,128)} %param.13) | copy-start | bytes 24580
  8.8 94.8 %all-gather.9.cloned.1.call-start = ((), (), s32[]{:S(2)}) async-start(), calls=%async_computation.2 | async-start | bytes 7077888 | tf_op jit(solution)/shard_map/all_gather | solution.py:90
  36.5 265.8 %all-gather.17.cloned.1.call-start = ((), (), s32[]{:S(2)}) async-start(), calls=%async_computation.6 | async-start | bytes 2359296 | tf_op jit(solution)/shard_map/all_gather | solution.py:110
  55.5 269.4 %all-gather.13.cloned.1.call-start = ((), (), s32[]{:S(2)}) async-start(), calls=%async_computation.4 | async-start | bytes 12976128 | tf_op jit(solution)/shard_map/all_gather | solution.py:123
  131.1 5.1 %copy-start.4 = (bf16[704,128]{1,0:T(8,128)(2,1)S(1)}, bf16[704,128]{1,0:T(8,128)(2,1)}, u32[]{:S(2)}) copy-start(bf16[704,128]{1,0:T(8,128)(2,1)} %param.18) | copy-start | bytes 540676
  131.1 111.8 %copy-start.6 = (s32[512]{0:T(512)S(1)}, s32[512]{0:T(512)}, u32[]{:S(2)}) copy-start(s32[512]{0:T(512)} %param.20) | copy-start | bytes 6148
  131.1 123.8 %copy-start.7 = (s32[512]{0:T(512)S(1)}, s32[512]{0:T(512)}, u32[]{:S(2)}) copy-start(s32[512]{0:T(512)} %param.19) | copy-start | bytes 6148
  131.1 136.0 %all-to-all-start = ((bf16[3,512,1024]{1,0,2:T(4,128)(2,1)}), bf16[3,512,1024]{1,0,2:T(4,128)(2,1)}, u32[]{:S(2)}, u32[]{:S(2)}) async-start(bf16[3,512,1024]{1,0,2:T(4,128)(2,1)} %copy.49), calls=%async_computation | async-start | bytes 8388608 | tf_op jit(solution)/shard_map/all_to_all | solution.py:96
  136.1 202.1 %all-gather.15.cloned.1.call-start = ((), (), s32[]{:S(2)}) async-start(), calls=%async_computation.5 | async-start | bytes 6488064 | tf_op jit(solution)/shard_map/all_gather | solution.py:130
  298.5 22.4 %all-to-all-start.1 = ((bf16[4,512,256]{1,2,0:T(8,128)(2,1)}), bf16[4,512,256]{1,2,0:T(8,128)(2,1)S(1)}, u32[]{:S(2)}, u32[]{:S(2)}) async-start(bf16[4,512,256]{1,2,0:T(8,128)(2,1)} %bitcast.24), calls=%async_computation.1 | async-start | bytes 2097152 | tf_op jit(solution)/shard_map/all_to_all | solution.py:106
  320.9 1.0 copy-start.3
  338.2 10.2 %copy-start.1 = (f32[2,16]{1,0:T(2,128)S(1)}, f32[2,16]{1,0:T(2,128)}, u32[]{:S(2)}) copy-start(f32[2,16]{1,0:T(2,128)} %param.16) | copy-start | bytes 388
Sparse Core Ops, SparseCore 0:
  8.9 47.8 all-gather.10
  58.7 44.7 all-gather.8
  105.4 27.7 all-gather.16
  135.0 67.5 all-gather.12
  243.0 44.1 all-gather.14
